TPU v7x, 32 devices: a whole 2x2x4 slice. The times are simulated.
32 devices in a mesh: gx: 4 (over x, core), gy: 2 (over y), gz: 4 (over z).
Axes of the slice: x: 2, y: 2, z: 4, core: 2. Of those that a mesh axis runs over, the one named last changes fastest.
Arguments:
- positions: float32 [3, 4, 2, 4, 256], P(None, 'gx', 'gy', 'gz'), may hold values from 0 to 4, as said below
- velocities: float32 [3, 4, 2, 4, 256], P(None, 'gx', 'gy', 'gz'), may hold values from -6 to 6
- forces: float32 [3, 4, 2, 4, 256], P(None, 'gx', 'gy', 'gz'), may hold values from -6 to 6
- charges: float32 [4, 2, 4, 256], P('gx', 'gy', 'gz'), may hold values from -2 to 2
- inverse_mass: float32 [4, 2, 4, 256], P('gx', 'gy', 'gz'), may hold values from 0.5 to 2
- occupancy: int32 [4, 2, 4], P('gx', 'gy', 'gz'), may hold values from 128 to 256
- molecule: int32 [4, 2, 4, 256], P('gx', 'gy', 'gz'), may hold values from 0 to 127, never falling along the last dimension, each value on 1 to 4 neighbouring positions
Outputs:
- positions_out: float32 [3, 4, 2, 4, 256], P(None, 'gx', 'gy', 'gz')
- velocities_out: float32 [3, 4, 2, 4, 256], P(None, 'gx', 'gy', 'gz')
- forces_out: float32 [3, 4, 2, 4, 256], P(None, 'gx', 'gy', 'gz')
Inputs may be any that keep to these rules, and one draw needn't show every extreme that they name: `positions`: component c of a particle of the box with index k along dimension c lies in [k, k + 1).
All inputs are finite; a program needn't handle non-finite values.
Results may differ from a plain program's by a relative error of at most 0.0003.
Values sent between devices are 32-bit elements; how exact they have to be, the bound alone decides.
No kernel may reach another device: no remote copies, remote signals or barrier semaphores. Data moves between devices by JAX's collectives and lax.ppermute only.
A program may use at most 64 MiB of HBM per device.

v0:
```python
import jax
import jax.numpy as jnp
from jax import lax
from jax.sharding import PartitionSpec as P

cutoff_square = 4.0
soften_square = 0.25
time_step = 0.1
half_step = 0.05


def passed_along(block, axis, distance):
    devices = range(lax.axis_size(axis))
    route = [((i - distance) % len(devices), i) for i in devices]
    return lax.ppermute(block, axis, route)


def separations_of(target_places, source_places, lengths):
    separations = []
    for component in range(3):
        spacing = target_places[component][:, None] - source_places[component][None, :]
        separations.append(
            spacing - lengths[component] * jnp.floor(spacing / lengths[component] + 0.5)
        )
    squared = (
        separations[0] * separations[0]
        + separations[1] * separations[1]
        + separations[2] * separations[2]
    )
    switch = jnp.maximum(1.0 - squared / cutoff_square, 0.0)
    soften = squared + soften_square
    return (separations, switch * switch / (soften * jnp.sqrt(soften)))


def interact(target_places, target_charge, source_places, source_charge, lengths, pair_mask):
    separations, base = separations_of(target_places, source_places, lengths)
    weight = source_charge[None, :] * base
    if pair_mask is not None:
        weight = weight * pair_mask
    return jnp.stack(
        [target_charge * jnp.sum(weight * separation, axis=-1) for separation in separations]
    )


def cycle_offsets(cycle_size):
    if cycle_size >= 5:
        return [1, -1, 2, -2]
    return list(range(1, cycle_size))


def across_second(gathered):
    pieces = [gathered]
    for offset in cycle_offsets(lax.axis_size("gy")):
        pieces.append(passed_along(gathered, "gy", offset))
    return jnp.stack(pieces)


def across_first(gathered):
    pieces = [gathered]
    for offset in cycle_offsets(lax.axis_size("gx")):
        pieces.append(passed_along(gathered, "gx", offset))
    return jnp.stack(pieces)


def forward_sum(summed, places, charge_live, blocks, lengths):

    def advance(total, column):
        return (total + interact(places, charge_live, column[:3], column[3], lengths, None), None)

    result, unused = lax.scan(advance, summed, blocks)
    return result


def full_shell(places, charge_live, tower_data, lengths):
    stacked = across_first(across_second(tower_data))
    blocks = stacked.reshape(-1, 4, tower_data.shape[1])
    return forward_sum(jnp.zeros_like(places), places, charge_live, blocks, lengths)


def force_field(places, charge_live, same_molecule, lengths):
    sources = jnp.concatenate([places, charge_live[None]], axis=0)
    tower_data = lax.all_gather(sources, "gz", axis=1, tiled=True)
    summed = full_shell(places, charge_live, tower_data, lengths)
    return summed - interact(places, charge_live, places, charge_live, lengths, same_molecule)


def local(positions, velocities, forces, charges, inverse_mass, occupancy, molecule):
    lengths = (float(lax.axis_size("gx")), float(lax.axis_size("gy")), float(lax.axis_size("gz")))
    shape = positions.shape
    places = positions.reshape(3, -1)
    velocity = velocities.reshape(3, -1)
    current = forces.reshape(3, -1)
    slots_count = places.shape[1]
    slots = jnp.arange(slots_count, dtype=jnp.int32)
    charge_live = jnp.where(slots < occupancy.reshape(()), charges.reshape(-1), jnp.float32(0.0))
    mass_inverse = inverse_mass.reshape(-1)
    labels = molecule.reshape(-1)
    same_molecule = (labels[:, None] == labels[None, :]).astype(jnp.float32)
    for turn in range(2):
        midway = velocity + half_step * mass_inverse * current
        places = places + time_step * midway
        current = force_field(places, charge_live, same_molecule, lengths)
        velocity = midway + half_step * mass_inverse * current
    return (places.reshape(shape), velocity.reshape(shape), current.reshape(shape))


def solution(mesh):
    in_specs = (
        P(None, "gx", "gy", "gz", None),
        P(None, "gx", "gy", "gz", None),
        P(None, "gx", "gy", "gz", None),
        P("gx", "gy", "gz", None),
        P("gx", "gy", "gz", None),
        P("gx", "gy", "gz"),
        P("gx", "gy", "gz", None),
    )
    out_specs = (
        P(None, "gx", "gy", "gz", None),
        P(None, "gx", "gy", "gz", None),
        P(None, "gx", "gy", "gz", None),
    )
    return jax.shard_map(local, mesh=mesh, in_specs=in_specs, out_specs=out_specs, check_vma=False)
```

profile of v0, /device:TPU:1, one launch (start us, length us, event | category | flops | bytes accessed | tf_op | source)
XLA Modules:
  0.0 84.3 jit_solution(9478626252136731197)
XLA Ops:
  4.7 11.4 %all_gather.6 = f32[4,1024]{1,0:T(4,128)S(1)} all-gather(f32[4,256]{1,0:T(4,128)S(1)} %pad_maximum_fusion.5), channel_id=1, replica_groups=mesh['gx'=4,'gy'=2,'gz'=4] {'gz'}, dimensions={1}, use_global_device_ids=true | all-gather | bytes 20480 | tf_op jit(solution)/shard_map/all_gather | solution.py:82
  19.0 5.6 %collective-permute-start.1 = (f32[2,4,1024]{2,1,0:T(4,128)S(1)}, f32[2,4,1024]{2,1,0:T(4,128)S(1)}, u32[]{:S(2)}, u32[]{:S(2)}) collective-permute-start(f32[2,4,1024]{2,1,0:T(4,128)S(1)} %get-tuple-element.156), channel_id=1, source_target_pairs={{24,0},{0,8},{8,16},{16,24},{25,1},{1,9},{9,17},{17,25},{26,2},{2,... | collective-permute-start | bytes 98312 | tf_op jit(solution)/shard_map/ppermute | solution.py:15
  25.6 1.7 %collective-permute-done.2 = f32[2,4,1024]{2,1,0:T(4,128)S(1)} collective-permute-done((f32[2,4,1024]{2,1,0:T(4,128)S(1)}, f32[2,4,1024]{2,1,0:T(4,128)S(1)}, u32[]{:S(2)}, u32[]{:S(2)}) %collective-permute-start.2) | collective-permute-done | bytes 32800 | tf_op jit(solution)/shard_map/ppermute | solution.py:15
  28.2 16.3 %while.22 = (s32[]{:T(128)}, f32[3,256]{1,0:T(4,128)S(1)}, f32[8,4,1024]{2,1,0:T(4,128)S(1)}, f32[3,256]{1,0:T(4,128)S(1)}, f32[256]{0:T(256)S(1)}, /*index=5*/s32[]{:T(128)}, s32[]{:T(128)}, s32[]{}, s32[]{}, s32[]{}) while((s32[]{:T(128)}, f32[3,256]{1,0:T(4,128)S(1)}, f32[8,4,1024]{2,1,0:T(4,128)S(1)}, f32[3,256]{1,0:T(4,128)S(1)}, ...), condition=%wide.region_4.5_spmd.clone, body=%wide.region_0.4_spmd.clone.sunk | while | flops 9702406 | bytes 77987 | solution.py:70
  28.3 1.9 %fusion.108 = (f32[256]{0:T(256)S(1)}, f32[256]{0:T(256)S(1)}, f32[256]{0:T(256)S(1)}) fusion(f32[1024]{0:T(1024)S(1)} %bitcast.119, f32[256]{0:T(256)S(1)} %bitcast.141, f32[1024]{0:T(1024)S(1)} %bitcast.120, f32[256]{0:T(256)S(1)} %bitcast.140, f32[1024]{0:T(1024)S(1)} %bitcast.118, f32[256]{0:T(256)S(1)} %bitcast.139, f32[1024]{0:T(1024)S(1)} %bitcast.117), kind=kLoop, calls=%fused_computation.14.clone.1 | loop fusion | flops 9698560 | bytes 22528 | tf_op jit(solution)/shard_map/while/body/eval_jaxpr/reduce_sum | solution.py:41
  30.3 1.9 %fusion.108 = (f32[256]{0:T(256)S(1)}, f32[256]{0:T(256)S(1)}, f32[256]{0:T(256)S(1)}) fusion(f32[1024]{0:T(1024)S(1)} %bitcast.119, f32[256]{0:T(256)S(1)} %bitcast.141, f32[1024]{0:T(1024)S(1)} %bitcast.120, f32[256]{0:T(256)S(1)} %bitcast.140, f32[1024]{0:T(1024)S(1)} %bitcast.118, f32[256]{0:T(256)S(1)} %bitcast.139, f32[1024]{0:T(1024)S(1)} %bitcast.117), kind=kLoop, calls=%fused_computation.14.clone.1 | loop fusion | flops 9698560 | bytes 22528 | tf_op jit(solution)/shard_map/while/body/eval_jaxpr/reduce_sum | solution.py:41
  32.3 1.9 %fusion.108 = (f32[256]{0:T(256)S(1)}, f32[256]{0:T(256)S(1)}, f32[256]{0:T(256)S(1)}) fusion(f32[1024]{0:T(1024)S(1)} %bitcast.119, f32[256]{0:T(256)S(1)} %bitcast.141, f32[1024]{0:T(1024)S(1)} %bitcast.120, f32[256]{0:T(256)S(1)} %bitcast.140, f32[1024]{0:T(1024)S(1)} %bitcast.118, f32[256]{0:T(256)S(1)} %bitcast.139, f32[1024]{0:T(1024)S(1)} %bitcast.117), kind=kLoop, calls=%fused_computation.14.clone.1 | loop fusion | flops 9698560 | bytes 22528 | tf_op jit(solution)/shard_map/while/body/eval_jaxpr/reduce_sum | solution.py:41
  34.4 1.9 %fusion.108 = (f32[256]{0:T(256)S(1)}, f32[256]{0:T(256)S(1)}, f32[256]{0:T(256)S(1)}) fusion(f32[1024]{0:T(1024)S(1)} %bitcast.119, f32[256]{0:T(256)S(1)} %bitcast.141, f32[1024]{0:T(1024)S(1)} %bitcast.120, f32[256]{0:T(256)S(1)} %bitcast.140, f32[1024]{0:T(1024)S(1)} %bitcast.118, f32[256]{0:T(256)S(1)} %bitcast.139, f32[1024]{0:T(1024)S(1)} %bitcast.117), kind=kLoop, calls=%fused_computation.14.clone.1 | loop fusion | flops 9698560 | bytes 22528 | tf_op jit(solution)/shard_map/while/body/eval_jaxpr/reduce_sum | solution.py:41
  36.4 1.9 %fusion.108 = (f32[256]{0:T(256)S(1)}, f32[256]{0:T(256)S(1)}, f32[256]{0:T(256)S(1)}) fusion(f32[1024]{0:T(1024)S(1)} %bitcast.119, f32[256]{0:T(256)S(1)} %bitcast.141, f32[1024]{0:T(1024)S(1)} %bitcast.120, f32[256]{0:T(256)S(1)} %bitcast.140, f32[1024]{0:T(1024)S(1)} %bitcast.118, f32[256]{0:T(256)S(1)} %bitcast.139, f32[1024]{0:T(1024)S(1)} %bitcast.117), kind=kLoop, calls=%fused_computation.14.clone.1 | loop fusion | flops 9698560 | bytes 22528 | tf_op jit(solution)/shard_map/while/body/eval_jaxpr/reduce_sum | solution.py:41
  38.4 1.9 %fusion.108 = (f32[256]{0:T(256)S(1)}, f32[256]{0:T(256)S(1)}, f32[256]{0:T(256)S(1)}) fusion(f32[1024]{0:T(1024)S(1)} %bitcast.119, f32[256]{0:T(256)S(1)} %bitcast.141, f32[1024]{0:T(1024)S(1)} %bitcast.120, f32[256]{0:T(256)S(1)} %bitcast.140, f32[1024]{0:T(1024)S(1)} %bitcast.118, f32[256]{0:T(256)S(1)} %bitcast.139, f32[1024]{0:T(1024)S(1)} %bitcast.117), kind=kLoop, calls=%fused_computation.14.clone.1 | loop fusion | flops 9698560 | bytes 22528 | tf_op jit(solution)/shard_map/while/body/eval_jaxpr/reduce_sum | solution.py:41
  40.5 1.9 %fusion.108 = (f32[256]{0:T(256)S(1)}, f32[256]{0:T(256)S(1)}, f32[256]{0:T(256)S(1)}) fusion(f32[1024]{0:T(1024)S(1)} %bitcast.119, f32[256]{0:T(256)S(1)} %bitcast.141, f32[1024]{0:T(1024)S(1)} %bitcast.120, f32[256]{0:T(256)S(1)} %bitcast.140, f32[1024]{0:T(1024)S(1)} %bitcast.118, f32[256]{0:T(256)S(1)} %bitcast.139, f32[1024]{0:T(1024)S(1)} %bitcast.117), kind=kLoop, calls=%fused_computation.14.clone.1 | loop fusion | flops 9698560 | bytes 22528 | tf_op jit(solution)/shard_map/while/body/eval_jaxpr/reduce_sum | solution.py:41
  42.5 1.9 %fusion.108 = (f32[256]{0:T(256)S(1)}, f32[256]{0:T(256)S(1)}, f32[256]{0:T(256)S(1)}) fusion(f32[1024]{0:T(1024)S(1)} %bitcast.119, f32[256]{0:T(256)S(1)} %bitcast.141, f32[1024]{0:T(1024)S(1)} %bitcast.120, f32[256]{0:T(256)S(1)} %bitcast.140, f32[1024]{0:T(1024)S(1)} %bitcast.118, f32[256]{0:T(256)S(1)} %bitcast.139, f32[1024]{0:T(1024)S(1)} %bitcast.117), kind=kLoop, calls=%fused_computation.14.clone.1 | loop fusion | flops 9698560 | bytes 22528 | tf_op jit(solution)/shard_map/while/body/eval_jaxpr/reduce_sum | solution.py:41
  45.2 10.3 %all_gather.7 = f32[4,1024]{1,0:T(4,128)S(1)} all-gather(f32[4,256]{1,0:T(4,128)S(1)} %pad_maximum_fusion.4), channel_id=1, replica_groups=mesh['gx'=4,'gy'=2,'gz'=4] {'gz'}, dimensions={1}, use_global_device_ids=true | all-gather | bytes 20480 | tf_op jit(solution)/shard_map/all_gather | solution.py:82
  58.2 4.5 %collective-permute-start.5 = (f32[2,4,1024]{2,1,0:T(4,128)S(1)}, f32[2,4,1024]{2,1,0:T(4,128)S(1)}, u32[]{:S(2)}, u32[]{:S(2)}) collective-permute-start(f32[2,4,1024]{2,1,0:T(4,128)S(1)} %get-tuple-element.154), channel_id=1, source_target_pairs={{24,0},{0,8},{8,16},{16,24},{25,1},{1,9},{9,17},{17,25},{26,2},{2,... | collective-permute-start | bytes 98312 | tf_op jit(solution)/shard_map/ppermute | solution.py:15
  64.0 2.0 %collective-permute-done.6 = f32[2,4,1024]{2,1,0:T(4,128)S(1)} collective-permute-done((f32[2,4,1024]{2,1,0:T(4,128)S(1)}, f32[2,4,1024]{2,1,0:T(4,128)S(1)}, u32[]{:S(2)}, u32[]{:S(2)}) %collective-permute-start.6) | collective-permute-done | bytes 32800 | tf_op jit(solution)/shard_map/ppermute | solution.py:15
  66.8 16.3 %while.23 = (s32[]{:T(128)}, f32[3,256]{1,0:T(4,128)S(1)}, f32[8,4,1024]{2,1,0:T(4,128)S(1)}, f32[3,256]{1,0:T(4,128)S(1)}, f32[256]{0:T(256)S(1)}, /*index=5*/s32[]{:T(128)}, s32[]{:T(128)}, s32[]{}, s32[]{}, s32[]{}) while((s32[]{:T(128)}, f32[3,256]{1,0:T(4,128)S(1)}, f32[8,4,1024]{2,1,0:T(4,128)S(1)}, ...), condition=%wide.region_12.13_spmd.clone, body=%wide.region_8.12_spmd.clone.sunk | while | flops 9702406 | bytes 77987 | solution.py:70
  66.9 1.9 %fusion.111 = (f32[256]{0:T(256)S(1)}, f32[256]{0:T(256)S(1)}, f32[256]{0:T(256)S(1)}) fusion(f32[1024]{0:T(1024)S(1)} %bitcast.123, f32[256]{0:T(256)S(1)} %bitcast.144, f32[1024]{0:T(1024)S(1)} %bitcast.124, f32[256]{0:T(256)S(1)} %bitcast.143, f32[1024]{0:T(1024)S(1)} %bitcast.122, f32[256]{0:T(256)S(1)} %bitcast.142, f32[1024]{0:T(1024)S(1)} %bitcast.121), kind=kLoop, calls=%fused_computation.48.clone.1 | loop fusion | flops 9698560 | bytes 22528 | tf_op jit(solution)/shard_map/while/body/eval_jaxpr/reduce_sum | solution.py:41
  68.9 1.9 %fusion.111 = (f32[256]{0:T(256)S(1)}, f32[256]{0:T(256)S(1)}, f32[256]{0:T(256)S(1)}) fusion(f32[1024]{0:T(1024)S(1)} %bitcast.123, f32[256]{0:T(256)S(1)} %bitcast.144, f32[1024]{0:T(1024)S(1)} %bitcast.124, f32[256]{0:T(256)S(1)} %bitcast.143, f32[1024]{0:T(1024)S(1)} %bitcast.122, f32[256]{0:T(256)S(1)} %bitcast.142, f32[1024]{0:T(1024)S(1)} %bitcast.121), kind=kLoop, calls=%fused_computation.48.clone.1 | loop fusion | flops 9698560 | bytes 22528 | tf_op jit(solution)/shard_map/while/body/eval_jaxpr/reduce_sum | solution.py:41
  71.0 1.9 %fusion.111 = (f32[256]{0:T(256)S(1)}, f32[256]{0:T(256)S(1)}, f32[256]{0:T(256)S(1)}) fusion(f32[1024]{0:T(1024)S(1)} %bitcast.123, f32[256]{0:T(256)S(1)} %bitcast.144, f32[1024]{0:T(1024)S(1)} %bitcast.124, f32[256]{0:T(256)S(1)} %bitcast.143, f32[1024]{0:T(1024)S(1)} %bitcast.122, f32[256]{0:T(256)S(1)} %bitcast.142, f32[1024]{0:T(1024)S(1)} %bitcast.121), kind=kLoop, calls=%fused_computation.48.clone.1 | loop fusion | flops 9698560 | bytes 22528 | tf_op jit(solution)/shard_map/while/body/eval_jaxpr/reduce_sum | solution.py:41
  73.0 1.9 %fusion.111 = (f32[256]{0:T(256)S(1)}, f32[256]{0:T(256)S(1)}, f32[256]{0:T(256)S(1)}) fusion(f32[1024]{0:T(1024)S(1)} %bitcast.123, f32[256]{0:T(256)S(1)} %bitcast.144, f32[1024]{0:T(1024)S(1)} %bitcast.124, f32[256]{0:T(256)S(1)} %bitcast.143, f32[1024]{0:T(1024)S(1)} %bitcast.122, f32[256]{0:T(256)S(1)} %bitcast.142, f32[1024]{0:T(1024)S(1)} %bitcast.121), kind=kLoop, calls=%fused_computation.48.clone.1 | loop fusion | flops 9698560 | bytes 22528 | tf_op jit(solution)/shard_map/while/body/eval_jaxpr/reduce_sum | solution.py:41
  75.0 1.9 %fusion.111 = (f32[256]{0:T(256)S(1)}, f32[256]{0:T(256)S(1)}, f32[256]{0:T(256)S(1)}) fusion(f32[1024]{0:T(1024)S(1)} %bitcast.123, f32[256]{0:T(256)S(1)} %bitcast.144, f32[1024]{0:T(1024)S(1)} %bitcast.124, f32[256]{0:T(256)S(1)} %bitcast.143, f32[1024]{0:T(1024)S(1)} %bitcast.122, f32[256]{0:T(256)S(1)} %bitcast.142, f32[1024]{0:T(1024)S(1)} %bitcast.121), kind=kLoop, calls=%fused_computation.48.clone.1 | loop fusion | flops 9698560 | bytes 22528 | tf_op jit(solution)/shard_map/while/body/eval_jaxpr/reduce_sum | solution.py:41
  77.1 1.9 %fusion.111 = (f32[256]{0:T(256)S(1)}, f32[256]{0:T(256)S(1)}, f32[256]{0:T(256)S(1)}) fusion(f32[1024]{0:T(1024)S(1)} %bitcast.123, f32[256]{0:T(256)S(1)} %bitcast.144, f32[1024]{0:T(1024)S(1)} %bitcast.124, f32[256]{0:T(256)S(1)} %bitcast.143, f32[1024]{0:T(1024)S(1)} %bitcast.122, f32[256]{0:T(256)S(1)} %bitcast.142, f32[1024]{0:T(1024)S(1)} %bitcast.121), kind=kLoop, calls=%fused_computation.48.clone.1 | loop fusion | flops 9698560 | bytes 22528 | tf_op jit(solution)/shard_map/while/body/eval_jaxpr/reduce_sum | solution.py:41
  79.1 1.9 %fusion.111 = (f32[256]{0:T(256)S(1)}, f32[256]{0:T(256)S(1)}, f32[256]{0:T(256)S(1)}) fusion(f32[1024]{0:T(1024)S(1)} %bitcast.123, f32[256]{0:T(256)S(1)} %bitcast.144, f32[1024]{0:T(1024)S(1)} %bitcast.124, f32[256]{0:T(256)S(1)} %bitcast.143, f32[1024]{0:T(1024)S(1)} %bitcast.122, f32[256]{0:T(256)S(1)} %bitcast.142, f32[1024]{0:T(1024)S(1)} %bitcast.121), kind=kLoop, calls=%fused_computation.48.clone.1 | loop fusion | flops 9698560 | bytes 22528 | tf_op jit(solution)/shard_map/while/body/eval_jaxpr/reduce_sum | solution.py:41
  81.1 1.9 %fusion.111 = (f32[256]{0:T(256)S(1)}, f32[256]{0:T(256)S(1)}, f32[256]{0:T(256)S(1)}) fusion(f32[1024]{0:T(1024)S(1)} %bitcast.123, f32[256]{0:T(256)S(1)} %bitcast.144, f32[1024]{0:T(1024)S(1)} %bitcast.124, f32[256]{0:T(256)S(1)} %bitcast.143, f32[1024]{0:T(1024)S(1)} %bitcast.122, f32[256]{0:T(256)S(1)} %bitcast.142, f32[1024]{0:T(1024)S(1)} %bitcast.121), kind=kLoop, calls=%fused_computation.48.clone.1 | loop fusion | flops 9698560 | bytes 22528 | tf_op jit(solution)/shard_map/while/body/eval_jaxpr/reduce_sum | solution.py:41
  (107 shorter events, 15.8 us)
Async XLA Ops:
  0.6 0.7 copy-start
  2.7 0.7 copy-start.2
  3.4 0.7 copy-start.3
  16.1 2.9 %collective-permute-start = (f32[4,1024]{1,0:T(4,128)S(1)}, f32[4,1024]{1,0:T(4,128)S(1)}, u32[]{:S(2)}, u32[]{:S(2)}) collective-permute-start(f32[4,1024]{1,0:T(4,128)S(1)} %all_gather.6), channel_id=1, source_target_pairs={{4,0},{0,4},{5,1},{1,5},{6,2},{2,6},{7,3},{3,7},{12,8},{8,12},{13,... | collective-permute-start | bytes 49160 | tf_op jit(solution)/shard_map/ppermute | solution.py:15
  19.0 6.6 %collective-permute-start.1 = (f32[2,4,1024]{2,1,0:T(4,128)S(1)}, f32[2,4,1024]{2,1,0:T(4,128)S(1)}, u32[]{:S(2)}, u32[]{:S(2)}) collective-permute-start(f32[2,4,1024]{2,1,0:T(4,128)S(1)} %get-tuple-element.156), channel_id=1, source_target_pairs={{24,0},{0,8},{8,16},{16,24},{25,1},{1,9},{9,17},{17,25},{26,2},{2,... | collective-permute-start | bytes 98312 | tf_op jit(solution)/shard_map/ppermute | solution.py:15
  24.6 2.8 %collective-permute-start.2 = (f32[2,4,1024]{2,1,0:T(4,128)S(1)}, f32[2,4,1024]{2,1,0:T(4,128)S(1)}, u32[]{:S(2)}, u32[]{:S(2)}) collective-permute-start(f32[2,4,1024]{2,1,0:T(4,128)S(1)} %get-tuple-element.156), channel_id=1, source_target_pairs={{16,0},{24,8},{0,16},{8,24},{17,1},{25,9},{1,17},{9,25},{18,2},{26... | collective-permute-start | bytes 98312 | tf_op jit(solution)/shard_map/ppermute | solution.py:15
  24.8 3.3 %collective-permute-start.3 = (f32[2,4,1024]{2,1,0:T(4,128)S(1)}, f32[2,4,1024]{2,1,0:T(4,128)S(1)}, u32[]{:S(2)}, u32[]{:S(2)}) collective-permute-start(f32[2,4,1024]{2,1,0:T(4,128)S(1)} %get-tuple-element.156), channel_id=1, source_target_pairs={{8,0},{16,8},{24,16},{0,24},{9,1},{17,9},{25,17},{1,25},{10,2},{18... | collective-permute-start | bytes 98312 | tf_op jit(solution)/shard_map/ppermute | solution.py:15
  44.5 0.7 copy-start.1
  55.5 2.6 %collective-permute-start.4 = (f32[4,1024]{1,0:T(4,128)S(1)}, f32[4,1024]{1,0:T(4,128)S(1)}, u32[]{:S(2)}, u32[]{:S(2)}) collective-permute-start(f32[4,1024]{1,0:T(4,128)S(1)} %all_gather.7), channel_id=1, source_target_pairs={{4,0},{0,4},{5,1},{1,5},{6,2},{2,6},{7,3},{3,7},{12,8},{8,12},{13,... | collective-permute-start | bytes 49160 | tf_op jit(solution)/shard_map/ppermute | solution.py:15
  58.2 5.9 %collective-permute-start.5 = (f32[2,4,1024]{2,1,0:T(4,128)S(1)}, f32[2,4,1024]{2,1,0:T(4,128)S(1)}, u32[]{:S(2)}, u32[]{:S(2)}) collective-permute-start(f32[2,4,1024]{2,1,0:T(4,128)S(1)} %get-tuple-element.154), channel_id=1, source_target_pairs={{24,0},{0,8},{8,16},{16,24},{25,1},{1,9},{9,17},{17,25},{26,2},{2,... | collective-permute-start | bytes 98312 | tf_op jit(solution)/shard_map/ppermute | solution.py:15
  62.7 3.3 %collective-permute-start.6 = (f32[2,4,1024]{2,1,0:T(4,128)S(1)}, f32[2,4,1024]{2,1,0:T(4,128)S(1)}, u32[]{:S(2)}, u32[]{:S(2)}) collective-permute-start(f32[2,4,1024]{2,1,0:T(4,128)S(1)} %get-tuple-element.154), channel_id=1, source_target_pairs={{16,0},{24,8},{0,16},{8,24},{17,1},{25,9},{1,17},{9,25},{18,2},{26... | collective-permute-start | bytes 98312 | tf_op jit(solution)/shard_map/ppermute | solution.py:15
  63.5 3.3 %collective-permute-start.7 = (f32[2,4,1024]{2,1,0:T(4,128)S(1)}, f32[2,4,1024]{2,1,0:T(4,128)S(1)}, u32[]{:S(2)}, u32[]{:S(2)}) collective-permute-start(f32[2,4,1024]{2,1,0:T(4,128)S(1)} %get-tuple-element.154), channel_id=1, source_target_pairs={{8,0},{16,8},{24,16},{0,24},{9,1},{17,9},{25,17},{1,25},{10,2},{18... | collective-permute-start | bytes 98312 | tf_op jit(solution)/shard_map/ppermute | solution.py:15
where the time goes:
time: 84.6 us; the launch traced here: 84.3 us
  other arithmetic  34.2 us (40%)
  blocking collectives  21.7 us (26%)
  starting transfers between devices  13.8 us (16%)
  waiting for transfers between devices  8.21 us (10%)
  local copies, waits for them, and re-layouts  4.31 us (5%)
  between operations  1.39 us (2%)
    reduce_sum x18, other arithmetic, interact(): jnp.sum(weight * separation, axis=-1)  32.3 us
    all_gather x2, blocking collectives, force_field(): tower_data = lax.all_gather(sources, 'gz', axis=1, tiled=True)  21.7 us
    ppermute x8, starting transfers between devices, passed_along(): return lax.ppermute(block, axis, route)  13.8 us
    ppermute x8, waiting for transfers between devices, passed_along(): return lax.ppermute(block, axis, route)  8.21 us
    unnamed x8, local copies, waits for them, and re-layouts  2.04 us
  transfers between devices with their start and end apart: 8, of which 7 were waited for; matrix products, arithmetic and copies ran while one was open for 1% of the time, Pallas kernels for 0%

commit v1 on v0

--- a/solution.py
+++ b/solution.py
@@ -79,7 +79,12 @@
 
 def force_field(places, charge_live, same_molecule, lengths):
     sources = jnp.concatenate([places, charge_live[None]], axis=0)
-    tower_data = lax.all_gather(sources, "gz", axis=1, tiled=True)
+    ring = [sources]
+    for hop in range(3):
+        ring.append(lax.ppermute(ring[-1], "gz", [(dev, (dev + 1) % 4) for dev in range(4)]))
+    tower_data = jnp.roll(
+        jnp.concatenate(ring[::-1], axis=1), (lax.axis_index("gz") + 1) * ring[0].shape[1], axis=1
+    )
     summed = full_shell(places, charge_live, tower_data, lengths)
     return summed - interact(places, charge_live, places, charge_live, lengths, same_molecule)
 

time: 84.6 us -> 90.8 us (1.073)
  waiting for transfers between devices: 8.21 us -> 32.3 us
  blocking collectives: 21.7 us -> 0 us
  starting transfers between devices: 13.8 us -> 17.4 us
    ppermute x0 -> x6, waiting for transfers between devices: none -> 24.3 us  [force_field(): lax.ppermute(ring[-1], 'gz', [(dev, (dev + 1) % 4) for dev in range(4)])]
    all_gather x2 -> x0, blocking collectives: 21.7 us -> none  [force_field(): tower_data = lax.all_gather(sources, 'gz', axis=1, tiled=True)]
    ppermute x0 -> x6, starting transfers between devices: none -> 2.24 us  [force_field(): lax.ppermute(ring[-1], 'gz', [(dev, (dev + 1) % 4) for dev in range(4)])]
    ppermute x8, starting transfers between devices: 13.8 us -> 15.1 us  [passed_along(): return lax.ppermute(block, axis, route)]
  transfers between devices with their start and end apart: 8 -> 14, of which waited for: 7 -> 13; matrix products, arithmetic and copies ran while one was open for 1% -> 1% of each run, Pallas kernels for 0% -> 0%
where the time goes in v1:
time: 90.8 us; the launch traced here: 90.5 us
  other arithmetic  34.5 us (38%)
  waiting for transfers between devices  32.3 us (36%)
  starting transfers between devices  17.4 us (19%)
  local copies, waits for them, and re-layouts  4.28 us (5%)
  between operations  1.4 us (2%)
    reduce_sum x18, other arithmetic, interact(): jnp.sum(weight * separation, axis=-1)  32.3 us
    ppermute x6, waiting for transfers between devices, force_field(): lax.ppermute(ring[-1], 'gz', [(dev, (dev + 1) % 4) for dev in range(4)])  24.3 us
    ppermute x8, starting transfers between devices, passed_along(): return lax.ppermute(block, axis, route)  15.1 us
    ppermute x8, waiting for transfers between devices, passed_along(): return lax.ppermute(block, axis, route)  8.07 us
    ppermute x6, starting transfers between devices, force_field(): lax.ppermute(ring[-1], 'gz', [(dev, (dev + 1) % 4) for dev in range(4)])  2.24 us
    unnamed x8, local copies, waits for them, and re-layouts  2.04 us
  transfers between devices with their start and end apart: 14, of which 13 were waited for; matrix products, arithmetic and copies ran while one was open for 1% of the time, Pallas kernels for 0%

profile of v1, /device:TPU:1, one launch (start us, length us, event | category | flops | bytes accessed | tf_op | source)
XLA Modules:
  0.0 90.5 jit_solution(17285192098272769530)
XLA Ops:
  4.7 2.2 %collective-permute-start = (f32[4,256]{1,0:T(4,128)S(1)}, f32[4,256]{1,0:T(4,128)S(1)}, u32[]{:S(2)}, u32[]{:S(2)}) collective-permute-start(f32[4,256]{1,0:T(4,128)S(1)} %pad_maximum_fusion.5), channel_id=1, source_target_pairs={{0,1},{1,2},{2,3},{3,0},{4,5},{5,6},{6,7},{7,4},{8,9},{9,10},{10,1... | collective-permute-start | bytes 12296 | tf_op jit(solution)/shard_map/ppermute | solution.py:84
  6.9 3.0 %collective-permute-done = f32[4,256]{1,0:T(4,128)S(1)} collective-permute-done((f32[4,256]{1,0:T(4,128)S(1)}, f32[4,256]{1,0:T(4,128)S(1)}, u32[]{:S(2)}, u32[]{:S(2)}) %collective-permute-start) | collective-permute-done | bytes 4128 | tf_op jit(solution)/shard_map/ppermute | solution.py:84
  9.9 4.3 %collective-permute-done.1 = f32[4,256]{1,0:T(4,128)S(1)} collective-permute-done((f32[4,256]{1,0:T(4,128)S(1)}, f32[4,256]{1,0:T(4,128)S(1)}, u32[]{:S(2)}, u32[]{:S(2)}) %collective-permute-start.1) | collective-permute-done | bytes 4128 | tf_op jit(solution)/shard_map/ppermute | solution.py:84
  14.2 4.3 %collective-permute-done.2 = f32[4,256]{1,0:T(4,128)S(1)} collective-permute-done((f32[4,256]{1,0:T(4,128)S(1)}, f32[4,256]{1,0:T(4,128)S(1)}, u32[]{:S(2)}, u32[]{:S(2)}) %collective-permute-start.2) | collective-permute-done | bytes 4128 | tf_op jit(solution)/shard_map/ppermute | solution.py:84
  21.5 6.1 %collective-permute-start.4 = (f32[2,4,1024]{2,1,0:T(4,128)S(1)}, f32[2,4,1024]{2,1,0:T(4,128)S(1)}, u32[]{:S(2)}, u32[]{:S(2)}) collective-permute-start(f32[2,4,1024]{2,1,0:T(4,128)S(1)} %get-tuple-element.157), channel_id=1, source_target_pairs={{24,0},{0,8},{8,16},{16,24},{25,1},{1,9},{9,17},{17,25},{26,2},{2,... | collective-permute-start | bytes 98312 | tf_op jit(solution)/shard_map/ppermute | solution.py:15
  31.0 16.2 %while.22 = (s32[]{:T(128)}, f32[3,256]{1,0:T(4,128)S(1)}, f32[8,4,1024]{2,1,0:T(4,128)S(1)}, f32[3,256]{1,0:T(4,128)S(1)}, f32[256]{0:T(256)S(1)}, /*index=5*/s32[]{:T(128)}, s32[]{:T(128)}, s32[]{}, s32[]{}, s32[]{}) while((s32[]{:T(128)}, f32[3,256]{1,0:T(4,128)S(1)}, f32[8,4,1024]{2,1,0:T(4,128)S(1)}, f32[3,256]{1,0:T(4,128)S(1)}, ...), condition=%wide.region_4.6_spmd.clone, body=%wide.region_0.5_spmd.clone.sunk | while | flops 9702406 | bytes 77987 | solution.py:70
  31.1 1.9 %fusion.126 = (f32[256]{0:T(256)S(1)}, f32[256]{0:T(256)S(1)}, f32[256]{0:T(256)S(1)}) fusion(f32[1024]{0:T(1024)S(1)} %bitcast.119, f32[256]{0:T(256)S(1)} %bitcast.141, f32[1024]{0:T(1024)S(1)} %bitcast.120, f32[256]{0:T(256)S(1)} %bitcast.140, f32[1024]{0:T(1024)S(1)} %bitcast.118, f32[256]{0:T(256)S(1)} %bitcast.139, f32[1024]{0:T(1024)S(1)} %bitcast.117), kind=kLoop, calls=%fused_computation.14.clone.1 | loop fusion | flops 9698560 | bytes 22528 | tf_op jit(solution)/shard_map/while/body/eval_jaxpr/reduce_sum | solution.py:41
  33.1 1.9 %fusion.126 = (f32[256]{0:T(256)S(1)}, f32[256]{0:T(256)S(1)}, f32[256]{0:T(256)S(1)}) fusion(f32[1024]{0:T(1024)S(1)} %bitcast.119, f32[256]{0:T(256)S(1)} %bitcast.141, f32[1024]{0:T(1024)S(1)} %bitcast.120, f32[256]{0:T(256)S(1)} %bitcast.140, f32[1024]{0:T(1024)S(1)} %bitcast.118, f32[256]{0:T(256)S(1)} %bitcast.139, f32[1024]{0:T(1024)S(1)} %bitcast.117), kind=kLoop, calls=%fused_computation.14.clone.1 | loop fusion | flops 9698560 | bytes 22528 | tf_op jit(solution)/shard_map/while/body/eval_jaxpr/reduce_sum | solution.py:41
  37.2 1.9 %fusion.126 = (f32[256]{0:T(256)S(1)}, f32[256]{0:T(256)S(1)}, f32[256]{0:T(256)S(1)}) fusion(f32[1024]{0:T(1024)S(1)} %bitcast.119, f32[256]{0:T(256)S(1)} %bitcast.141, f32[1024]{0:T(1024)S(1)} %bitcast.120, f32[256]{0:T(256)S(1)} %bitcast.140, f32[1024]{0:T(1024)S(1)} %bitcast.118, f32[256]{0:T(256)S(1)} %bitcast.139, f32[1024]{0:T(1024)S(1)} %bitcast.117), kind=kLoop, calls=%fused_computation.14.clone.1 | loop fusion | flops 9698560 | bytes 22528 | tf_op jit(solution)/shard_map/while/body/eval_jaxpr/reduce_sum | solution.py:41
  43.3 1.9 %fusion.126 = (f32[256]{0:T(256)S(1)}, f32[256]{0:T(256)S(1)}, f32[256]{0:T(256)S(1)}) fusion(f32[1024]{0:T(1024)S(1)} %bitcast.119, f32[256]{0:T(256)S(1)} %bitcast.141, f32[1024]{0:T(1024)S(1)} %bitcast.120, f32[256]{0:T(256)S(1)} %bitcast.140, f32[1024]{0:T(1024)S(1)} %bitcast.118, f32[256]{0:T(256)S(1)} %bitcast.139, f32[1024]{0:T(1024)S(1)} %bitcast.117), kind=kLoop, calls=%fused_computation.14.clone.1 | loop fusion | flops 9698560 | bytes 22528 | tf_op jit(solution)/shard_map/while/body/eval_jaxpr/reduce_sum | solution.py:41
  48.1 4.2 %collective-permute-done.7 = f32[4,256]{1,0:T(4,128)S(1)} collective-permute-done((f32[4,256]{1,0:T(4,128)S(1)}, f32[4,256]{1,0:T(4,128)S(1)}, u32[]{:S(2)}, u32[]{:S(2)}) %collective-permute-start.7) | collective-permute-done | bytes 4128 | tf_op jit(solution)/shard_map/ppermute | solution.py:84
  52.3 4.3 %collective-permute-done.8 = f32[4,256]{1,0:T(4,128)S(1)} collective-permute-done((f32[4,256]{1,0:T(4,128)S(1)}, f32[4,256]{1,0:T(4,128)S(1)}, u32[]{:S(2)}, u32[]{:S(2)}) %collective-permute-start.8) | collective-permute-done | bytes 4128 | tf_op jit(solution)/shard_map/ppermute | solution.py:84
  56.6 4.2 %collective-permute-done.9 = f32[4,256]{1,0:T(4,128)S(1)} collective-permute-done((f32[4,256]{1,0:T(4,128)S(1)}, f32[4,256]{1,0:T(4,128)S(1)}, u32[]{:S(2)}, u32[]{:S(2)}) %collective-permute-start.9) | collective-permute-done | bytes 4128 | tf_op jit(solution)/shard_map/ppermute | solution.py:84
  63.9 5.0 %collective-permute-start.11 = (f32[2,4,1024]{2,1,0:T(4,128)S(1)}, f32[2,4,1024]{2,1,0:T(4,128)S(1)}, u32[]{:S(2)}, u32[]{:S(2)}) collective-permute-start(f32[2,4,1024]{2,1,0:T(4,128)S(1)} %get-tuple-element.155), channel_id=1, source_target_pairs={{24,0},{0,8},{8,16},{16,24},{25,1},{1,9},{9,17},{17,25},{26,2},{2,... | collective-permute-start | bytes 98312 | tf_op jit(solution)/shard_map/ppermute | solution.py:15
  70.3 2.0 %collective-permute-done.12 = f32[2,4,1024]{2,1,0:T(4,128)S(1)} collective-permute-done((f32[2,4,1024]{2,1,0:T(4,128)S(1)}, f32[2,4,1024]{2,1,0:T(4,128)S(1)}, u32[]{:S(2)}, u32[]{:S(2)}) %collective-permute-start.12) | collective-permute-done | bytes 32800 | tf_op jit(solution)/shard_map/ppermute | solution.py:15
  73.1 16.3 %while.23 = (s32[]{:T(128)}, f32[3,256]{1,0:T(4,128)S(1)}, f32[8,4,1024]{2,1,0:T(4,128)S(1)}, f32[3,256]{1,0:T(4,128)S(1)}, f32[256]{0:T(256)S(1)}, /*index=5*/s32[]{:T(128)}, s32[]{:T(128)}, s32[]{}, s32[]{}, s32[]{}) while((s32[]{:T(128)}, f32[3,256]{1,0:T(4,128)S(1)}, f32[8,4,1024]{2,1,0:T(4,128)S(1)}, ...), condition=%wide.region_12.14_spmd.clone, body=%wide.region_8.13_spmd.clone.sunk | while | flops 9702406 | bytes 77987 | solution.py:70
  73.1 1.9 %fusion.129 = (f32[256]{0:T(256)S(1)}, f32[256]{0:T(256)S(1)}, f32[256]{0:T(256)S(1)}) fusion(f32[1024]{0:T(1024)S(1)} %bitcast.123, f32[256]{0:T(256)S(1)} %bitcast.144, f32[1024]{0:T(1024)S(1)} %bitcast.124, f32[256]{0:T(256)S(1)} %bitcast.143, f32[1024]{0:T(1024)S(1)} %bitcast.122, f32[256]{0:T(256)S(1)} %bitcast.142, f32[1024]{0:T(1024)S(1)} %bitcast.121), kind=kLoop, calls=%fused_computation.48.clone.1 | loop fusion | flops 9698560 | bytes 22528 | tf_op jit(solution)/shard_map/while/body/eval_jaxpr/reduce_sum | solution.py:41
  75.2 1.9 %fusion.129 = (f32[256]{0:T(256)S(1)}, f32[256]{0:T(256)S(1)}, f32[256]{0:T(256)S(1)}) fusion(f32[1024]{0:T(1024)S(1)} %bitcast.123, f32[256]{0:T(256)S(1)} %bitcast.144, f32[1024]{0:T(1024)S(1)} %bitcast.124, f32[256]{0:T(256)S(1)} %bitcast.143, f32[1024]{0:T(1024)S(1)} %bitcast.122, f32[256]{0:T(256)S(1)} %bitcast.142, f32[1024]{0:T(1024)S(1)} %bitcast.121), kind=kLoop, calls=%fused_computation.48.clone.1 | loop fusion | flops 9698560 | bytes 22528 | tf_op jit(solution)/shard_map/while/body/eval_jaxpr/reduce_sum | solution.py:41
  77.2 1.9 %fusion.129 = (f32[256]{0:T(256)S(1)}, f32[256]{0:T(256)S(1)}, f32[256]{0:T(256)S(1)}) fusion(f32[1024]{0:T(1024)S(1)} %bitcast.123, f32[256]{0:T(256)S(1)} %bitcast.144, f32[1024]{0:T(1024)S(1)} %bitcast.124, f32[256]{0:T(256)S(1)} %bitcast.143, f32[1024]{0:T(1024)S(1)} %bitcast.122, f32[256]{0:T(256)S(1)} %bitcast.142, f32[1024]{0:T(1024)S(1)} %bitcast.121), kind=kLoop, calls=%fused_computation.48.clone.1 | loop fusion | flops 9698560 | bytes 22528 | tf_op jit(solution)/shard_map/while/body/eval_jaxpr/reduce_sum | solution.py:41
  79.2 1.9 %fusion.129 = (f32[256]{0:T(256)S(1)}, f32[256]{0:T(256)S(1)}, f32[256]{0:T(256)S(1)}) fusion(f32[1024]{0:T(1024)S(1)} %bitcast.123, f32[256]{0:T(256)S(1)} %bitcast.144, f32[1024]{0:T(1024)S(1)} %bitcast.124, f32[256]{0:T(256)S(1)} %bitcast.143, f32[1024]{0:T(1024)S(1)} %bitcast.122, f32[256]{0:T(256)S(1)} %bitcast.142, f32[1024]{0:T(1024)S(1)} %bitcast.121), kind=kLoop, calls=%fused_computation.48.clone.1 | loop fusion | flops 9698560 | bytes 22528 | tf_op jit(solution)/shard_map/while/body/eval_jaxpr/reduce_sum | solution.py:41
  81.3 1.9 %fusion.129 = (f32[256]{0:T(256)S(1)}, f32[256]{0:T(256)S(1)}, f32[256]{0:T(256)S(1)}) fusion(f32[1024]{0:T(1024)S(1)} %bitcast.123, f32[256]{0:T(256)S(1)} %bitcast.144, f32[1024]{0:T(1024)S(1)} %bitcast.124, f32[256]{0:T(256)S(1)} %bitcast.143, f32[1024]{0:T(1024)S(1)} %bitcast.122, f32[256]{0:T(256)S(1)} %bitcast.142, f32[1024]{0:T(1024)S(1)} %bitcast.121), kind=kLoop, calls=%fused_computation.48.clone.1 | loop fusion | flops 9698560 | bytes 22528 | tf_op jit(solution)/shard_map/while/body/eval_jaxpr/reduce_sum | solution.py:41
  83.3 1.9 %fusion.129 = (f32[256]{0:T(256)S(1)}, f32[256]{0:T(256)S(1)}, f32[256]{0:T(256)S(1)}) fusion(f32[1024]{0:T(1024)S(1)} %bitcast.123, f32[256]{0:T(256)S(1)} %bitcast.144, f32[1024]{0:T(1024)S(1)} %bitcast.124, f32[256]{0:T(256)S(1)} %bitcast.143, f32[1024]{0:T(1024)S(1)} %bitcast.122, f32[256]{0:T(256)S(1)} %bitcast.142, f32[1024]{0:T(1024)S(1)} %bitcast.121), kind=kLoop, calls=%fused_computation.48.clone.1 | loop fusion | flops 9698560 | bytes 22528 | tf_op jit(solution)/shard_map/while/body/eval_jaxpr/reduce_sum | solution.py:41
  85.3 1.9 %fusion.129 = (f32[256]{0:T(256)S(1)}, f32[256]{0:T(256)S(1)}, f32[256]{0:T(256)S(1)}) fusion(f32[1024]{0:T(1024)S(1)} %bitcast.123, f32[256]{0:T(256)S(1)} %bitcast.144, f32[1024]{0:T(1024)S(1)} %bitcast.124, f32[256]{0:T(256)S(1)} %bitcast.143, f32[1024]{0:T(1024)S(1)} %bitcast.122, f32[256]{0:T(256)S(1)} %bitcast.142, f32[1024]{0:T(1024)S(1)} %bitcast.121), kind=kLoop, calls=%fused_computation.48.clone.1 | loop fusion | flops 9698560 | bytes 22528 | tf_op jit(solution)/shard_map/while/body/eval_jaxpr/reduce_sum | solution.py:41
  87.4 1.9 %fusion.129 = (f32[256]{0:T(256)S(1)}, f32[256]{0:T(256)S(1)}, f32[256]{0:T(256)S(1)}) fusion(f32[1024]{0:T(1024)S(1)} %bitcast.123, f32[256]{0:T(256)S(1)} %bitcast.144, f32[1024]{0:T(1024)S(1)} %bitcast.124, f32[256]{0:T(256)S(1)} %bitcast.143, f32[1024]{0:T(1024)S(1)} %bitcast.122, f32[256]{0:T(256)S(1)} %bitcast.142, f32[1024]{0:T(1024)S(1)} %bitcast.121), kind=kLoop, calls=%fused_computation.48.clone.1 | loop fusion | flops 9698560 | bytes 22528 | tf_op jit(solution)/shard_map/while/body/eval_jaxpr/reduce_sum | solution.py:41
  (119 shorter events, 25.8 us)
Async XLA Ops:
  0.6 0.7 copy-start
  2.7 0.7 copy-start.2
  3.4 0.7 copy-start.3
  4.7 5.2 %collective-permute-start = (f32[4,256]{1,0:T(4,128)S(1)}, f32[4,256]{1,0:T(4,128)S(1)}, u32[]{:S(2)}, u32[]{:S(2)}) collective-permute-start(f32[4,256]{1,0:T(4,128)S(1)} %pad_maximum_fusion.5), channel_id=1, source_target_pairs={{0,1},{1,2},{2,3},{3,0},{4,5},{5,6},{6,7},{7,4},{8,9},{9,10},{10,1... | collective-permute-start | bytes 12296 | tf_op jit(solution)/shard_map/ppermute | solution.py:84
  9.9 4.3 %collective-permute-start.1 = (f32[4,256]{1,0:T(4,128)S(1)}, f32[4,256]{1,0:T(4,128)S(1)}, u32[]{:S(2)}, u32[]{:S(2)}) collective-permute-start(f32[4,256]{1,0:T(4,128)S(1)} %collective-permute-done), channel_id=1, source_target_pairs={{0,1},{1,2},{2,3},{3,0},{4,5},{5,6},{6,7},{7,4},{8,9},{9,10},{10,1... | collective-permute-start | bytes 12296 | tf_op jit(solution)/shard_map/ppermute | solution.py:84
  14.2 4.3 %collective-permute-start.2 = (f32[4,256]{1,0:T(4,128)S(1)}, f32[4,256]{1,0:T(4,128)S(1)}, u32[]{:S(2)}, u32[]{:S(2)}) collective-permute-start(f32[4,256]{1,0:T(4,128)S(1)} %collective-permute-done.1), channel_id=1, source_target_pairs={{0,1},{1,2},{2,3},{3,0},{4,5},{5,6},{6,7},{7,4},{8,9},{9,10},{10,1... | collective-permute-start | bytes 12296 | tf_op jit(solution)/shard_map/ppermute | solution.py:84
  18.6 2.9 %collective-permute-start.3 = (f32[4,1024]{1,0:T(4,128)S(1)}, f32[4,1024]{1,0:T(4,128)S(1)}, u32[]{:S(2)}, u32[]{:S(2)}) collective-permute-start(f32[4,1024]{1,0:T(4,128)S(1)} %fusion.100), channel_id=1, source_target_pairs={{4,0},{0,4},{5,1},{1,5},{6,2},{2,6},{7,3},{3,7},{12,8},{8,12},{13,... | collective-permute-start | bytes 49160 | tf_op jit(solution)/shard_map/ppermute | solution.py:15
  21.5 7.1 %collective-permute-start.4 = (f32[2,4,1024]{2,1,0:T(4,128)S(1)}, f32[2,4,1024]{2,1,0:T(4,128)S(1)}, u32[]{:S(2)}, u32[]{:S(2)}) collective-permute-start(f32[2,4,1024]{2,1,0:T(4,128)S(1)} %get-tuple-element.157), channel_id=1, source_target_pairs={{24,0},{0,8},{8,16},{16,24},{25,1},{1,9},{9,17},{17,25},{26,2},{2,... | collective-permute-start | bytes 98312 | tf_op jit(solution)/shard_map/ppermute | solution.py:15
  27.6 2.8 %collective-permute-start.5 = (f32[2,4,1024]{2,1,0:T(4,128)S(1)}, f32[2,4,1024]{2,1,0:T(4,128)S(1)}, u32[]{:S(2)}, u32[]{:S(2)}) collective-permute-start(f32[2,4,1024]{2,1,0:T(4,128)S(1)} %get-tuple-element.157), channel_id=1, source_target_pairs={{16,0},{24,8},{0,16},{8,24},{17,1},{25,9},{1,17},{9,25},{18,2},{26... | collective-permute-start | bytes 98312 | tf_op jit(solution)/shard_map/ppermute | solution.py:15
  27.6 3.3 %collective-permute-start.6 = (f32[2,4,1024]{2,1,0:T(4,128)S(1)}, f32[2,4,1024]{2,1,0:T(4,128)S(1)}, u32[]{:S(2)}, u32[]{:S(2)}) collective-permute-start(f32[2,4,1024]{2,1,0:T(4,128)S(1)} %get-tuple-element.157), channel_id=1, source_target_pairs={{8,0},{16,8},{24,16},{0,24},{9,1},{17,9},{25,17},{1,25},{10,2},{18... | collective-permute-start | bytes 98312 | tf_op jit(solution)/shard_map/ppermute | solution.py:15
  47.3 0.7 copy-start.1
  48.0 4.3 %collective-permute-start.7 = (f32[4,256]{1,0:T(4,128)S(1)}, f32[4,256]{1,0:T(4,128)S(1)}, u32[]{:S(2)}, u32[]{:S(2)}) collective-permute-start(f32[4,256]{1,0:T(4,128)S(1)} %pad_maximum_fusion.4), channel_id=1, source_target_pairs={{0,1},{1,2},{2,3},{3,0},{4,5},{5,6},{6,7},{7,4},{8,9},{9,10},{10,1... | collective-permute-start | bytes 12296 | tf_op jit(solution)/shard_map/ppermute | solution.py:84
  52.3 4.3 %collective-permute-start.8 = (f32[4,256]{1,0:T(4,128)S(1)}, f32[4,256]{1,0:T(4,128)S(1)}, u32[]{:S(2)}, u32[]{:S(2)}) collective-permute-start(f32[4,256]{1,0:T(4,128)S(1)} %collective-permute-done.7), channel_id=1, source_target_pairs={{0,1},{1,2},{2,3},{3,0},{4,5},{5,6},{6,7},{7,4},{8,9},{9,10},{10,1... | collective-permute-start | bytes 12296 | tf_op jit(solution)/shard_map/ppermute | solution.py:84
  56.6 4.3 %collective-permute-start.9 = (f32[4,256]{1,0:T(4,128)S(1)}, f32[4,256]{1,0:T(4,128)S(1)}, u32[]{:S(2)}, u32[]{:S(2)}) collective-permute-start(f32[4,256]{1,0:T(4,128)S(1)} %collective-permute-done.8), channel_id=1, source_target_pairs={{0,1},{1,2},{2,3},{3,0},{4,5},{5,6},{6,7},{7,4},{8,9},{9,10},{10,1... | collective-permute-start | bytes 12296 | tf_op jit(solution)/shard_map/ppermute | solution.py:84
  60.9 2.9 %collective-permute-start.10 = (f32[4,1024]{1,0:T(4,128)S(1)}, f32[4,1024]{1,0:T(4,128)S(1)}, u32[]{:S(2)}, u32[]{:S(2)}) collective-permute-start(f32[4,1024]{1,0:T(4,128)S(1)} %fusion.91), channel_id=1, source_target_pairs={{4,0},{0,4},{5,1},{1,5},{6,2},{2,6},{7,3},{3,7},{12,8},{8,12},{13,... | collective-permute-start | bytes 49160 | tf_op jit(solution)/shard_map/ppermute | solution.py:15
  63.9 6.4 %collective-permute-start.11 = (f32[2,4,1024]{2,1,0:T(4,128)S(1)}, f32[2,4,1024]{2,1,0:T(4,128)S(1)}, u32[]{:S(2)}, u32[]{:S(2)}) collective-permute-start(f32[2,4,1024]{2,1,0:T(4,128)S(1)} %get-tuple-element.155), channel_id=1, source_target_pairs={{24,0},{0,8},{8,16},{16,24},{25,1},{1,9},{9,17},{17,25},{26,2},{2,... | collective-permute-start | bytes 98312 | tf_op jit(solution)/shard_map/ppermute | solution.py:15
  68.9 3.3 %collective-permute-start.12 = (f32[2,4,1024]{2,1,0:T(4,128)S(1)}, f32[2,4,1024]{2,1,0:T(4,128)S(1)}, u32[]{:S(2)}, u32[]{:S(2)}) collective-permute-start(f32[2,4,1024]{2,1,0:T(4,128)S(1)} %get-tuple-element.155), channel_id=1, source_target_pairs={{16,0},{24,8},{0,16},{8,24},{17,1},{25,9},{1,17},{9,25},{18,2},{26... | collective-permute-start | bytes 98312 | tf_op jit(solution)/shard_map/ppermute | solution.py:15
  69.7 3.3 %collective-permute-start.13 = (f32[2,4,1024]{2,1,0:T(4,128)S(1)}, f32[2,4,1024]{2,1,0:T(4,128)S(1)}, u32[]{:S(2)}, u32[]{:S(2)}) collective-permute-start(f32[2,4,1024]{2,1,0:T(4,128)S(1)} %get-tuple-element.155), channel_id=1, source_target_pairs={{8,0},{16,8},{24,16},{0,24},{9,1},{17,9},{25,17},{1,25},{10,2},{18... | collective-permute-start | bytes 98312 | tf_op jit(solution)/shard_map/ppermute | solution.py:15
